TPU v7x, 32 devices: a whole 2x2x4 slice. The times are simulated.
32 devices in a mesh: tok: 16 (over z, x, core), blk: 2 (over y).
Axes of the slice: x: 2, y: 2, z: 4, core: 2. Of those that a mesh axis runs over, the one named last changes fastest.
Arguments:
- activations: bfloat16 [2048, 7168], P('tok', 'blk'), may hold values from -600 to 600
- signs: float32 [7168], P('blk'), may hold values from -1 to 1, as said below
Outputs:
- hessian: float32 [7168, 7168], P('tok', 'blk')
- incoherence: float32 [7168], P('blk')
- largest_ratio: float32 [], replicated
Inputs may be any that keep to these rules, and one draw needn't show every extreme that they name: `signs`: every entry is -1 or 1.
All inputs are finite; a program needn't handle non-finite values.
Results may differ from a plain program's by a relative error of at most 0.0037.
Values may be sent and summed in bfloat16 or wider, within the bound.
No kernel may reach another device: no remote copies, remote signals or barrier semaphores. Data moves between devices by JAX's collectives and lax.ppermute only.
A program may use at most 640 MiB of HBM per device.

v0:
```python
import math

import jax
import jax.numpy as jnp
from jax import lax
from jax.sharding import PartitionSpec as P

WALSH = 512
MIX = 14
FEATURES = 7168


EPS = 1e-06
DAMP = 0.01


def swapped(block, axis, distance):
    count = lax.axis_size(axis)
    route = []
    for low in range(count):
        high = low | 1 << distance
        if high != low and high < count:
            route += [(low, high), (high, low)]
    return lax.ppermute(block, axis, route)


def from_root(value, axis, source):
    kept = jnp.where(lax.axis_index(axis) == source, value, 0).astype(value.dtype)
    return lax.psum(kept, axis)


def walsh_table(length):
    position = jnp.arange(length, dtype=jnp.int32)
    parity = jnp.zeros((length, length), jnp.int32)
    for bit_number in range(length.bit_length() - 1):
        parity = parity + (position[:, None] >> bit_number & 1) * (
            position[None, :] >> bit_number & 1
        )
    return (1 - 2 * (parity % 2)).astype(jnp.float32)


def cosine_table(length):
    rows_idx = jnp.arange(length, dtype=jnp.float32)[:, None]
    columns = jnp.arange(length, dtype=jnp.float32)[None, :]
    table = math.sqrt(2.0 / length) * jnp.cos(math.pi * (columns + 0.5) * rows_idx / length)
    return jnp.where(rows_idx == 0.0, table * math.sqrt(0.5), table)


def contract_tokens(left, right):
    return lax.dot_general(
        left, right, (((0,), (0,)), ((), ())), preferred_element_type=jnp.float32
    )


def per_device(activations, signs):
    tok_rows, block_width = activations.shape
    blocks = lax.axis_size("blk")
    block_index = lax.axis_index("blk")
    token_groups = lax.axis_size("tok")
    token_index = lax.axis_index("tok")
    local_walsh = WALSH // blocks
    signed = activations * signs.astype(jnp.bfloat16)[None, :]
    local_table = jnp.kron(walsh_table(local_walsh) / math.sqrt(local_walsh), cosine_table(MIX).T)
    partial_mix = jnp.dot(signed.astype(jnp.float32), local_table, precision=lax.Precision.HIGHEST)
    for bit_number in range(blocks.bit_length() - 1):
        partner = swapped(partial_mix, "blk", bit_number)
        upper = block_index >> bit_number & 1 == 1
        partial_mix = jnp.where(upper, partner - partial_mix, partial_mix + partner)
    rotated = (partial_mix / math.sqrt(blocks)).astype(jnp.bfloat16)
    row_count = FEATURES // token_groups
    all_tokens = lax.all_gather(rotated, "tok", axis=0, tiled=True)
    first_row = token_index * row_count
    owner = first_row // block_width
    offset = first_row - owner * block_width
    own_slice = lax.dynamic_slice_in_dim(all_tokens, offset, row_count, 1)
    row_slice = from_root(own_slice, "blk", owner)
    gram_block = contract_tokens(row_slice, all_tokens)
    global_rows = token_index * row_count + jnp.arange(row_count, dtype=jnp.int32)[:, None]
    global_columns = block_index * block_width + jnp.arange(block_width, dtype=jnp.int32)[None, :]
    on_diag = global_rows == global_columns
    local_peaks = jnp.max(jnp.where(on_diag, 0.0, jnp.abs(gram_block)), axis=0)
    column_peak = lax.pmax(local_peaks, "tok")
    trace_total = lax.psum(jnp.sum(jnp.where(on_diag, gram_block, 0.0)), ("tok", "blk"))
    diag_mean = trace_total / FEATURES + EPS
    hessian = gram_block / diag_mean + DAMP * on_diag.astype(jnp.float32)
    incoherence = column_peak / diag_mean
    largest_ratio = lax.pmax(jnp.max(incoherence), "blk")
    return (hessian, incoherence, largest_ratio)


def solution(mesh):
    in_specs = (P("tok", "blk"), P("blk"))
    out_specs = (P("tok", "blk"), P("blk"), P())
    return jax.shard_map(
        per_device, mesh=mesh, in_specs=in_specs, out_specs=out_specs, check_vma=False
    )
```

profile of v0, /device:TPU:12, one launch (start us, length us, event | category | flops | bytes accessed | tf_op | source)
XLA Modules:
  0.0 860.5 jit_solution(9639242708453909916)
XLA Ops:
  7.2 0.0 all-gather.2.cloned.1.call-start
  7.3 0.1 multiply_select_fusion
  7.4 0.4 fusion.10
  7.8 142.1 %broadcast_multiply_fusion = f32[256,14,256,14]{3,2,1,0:T(8,128)} fusion(f32[14,14]{1,0:T(8,128)S(1)} %multiply_select_fusion, f32[256,256]{1,0:T(8,128)S(1)} %fusion.10), kind=kLoop, calls=%fused_computation | loop fusion | flops 12845056 | bytes 51643152 | tf_op jit(solution)/shard_map/jit(kron)/mul | solution.py:63
  149.9 0.0 copy-start.1
  149.9 0.0 copy-start
  149.9 326.1 %mul.279 = f32[3584,3584]{1,0:T(8,128)} reshape(f32[256,14,256,14]{3,2,1,0:T(8,128)} %broadcast_multiply_fusion) | data formatting | bytes 102760448 | tf_op jit(solution)/shard_map/jit(kron)/mul | solution.py:63
  476.0 0.0 copy-done.1
  476.0 0.0 copy-done
  476.0 24.3 %fusion.3 = f32[128,3584]{1,0:T(8,128)S(1)} fusion(f32[3584,3584]{1,0:T(8,128)} %mul.279, bf16[128,3584]{1,0:T(8,128)(2,1)S(1)} %copy-done, bf16[3584]{0:T(1024)(128)(2,1)S(1)} %convert_element_type.17), kind=kOutput, calls=%fused_computation.9 | convolution fusion | flops 19730464768 | bytes 54139904 | tf_op jit(solution)/shard_map/dot_general | solution.py:64
  500.3 0.6 collective-permute-start
  500.9 41.4 %collective-permute-done = f32[128,3584]{1,0:T(8,128)} collective-permute-done((f32[128,3584]{1,0:T(8,128)S(1)}, f32[128,3584]{1,0:T(8,128)}, u32[]{:S(2)}, u32[]{:S(2)}) %collective-permute-start) | collective-permute-done | bytes 1835040 | tf_op jit(solution)/shard_map/ppermute | solution.py:24
  542.2 2.7 multiply_convert_fusion
  544.9 0.0 all-gather.2.cloned.1.call-update
  545.0 0.2 all-reduce.2.cloned.1.call-start
  545.2 112.9 %all-gather.2.cloned.1.call-done = bf16[2048,3584]{1,0:T(8,128)(2,1)} async-done(((bf16[128,3584]{1,0:T(8,128)(2,1)}), bf16[2048,3584]{1,0:T(8,128)(2,1)}) %all-gather.2.cloned.1.call-update) | async-done | bytes 14680080 | tf_op jit(solution)/shard_map/all_gather | solution.py:71
  658.2 4.4 dynamic-slice_select_fusion
  662.6 0.0 all-reduce.2.cloned.1.call-update
  662.6 61.7 %all-reduce.2.cloned.1.call-done = bf16[2048,448]{1,0:T(8,128)(2,1)} async-done(((bf16[2048,448]{1,0:T(8,128)(2,1)}), bf16[2048,448]{1,0:T(8,128)(2,1)}) %all-reduce.2.cloned.1.call-update) | async-done | bytes 1835024 | tf_op jit(solution)/shard_map/psum | solution.py:29
  724.4 14.1 %fusion.2 = (f32[3584]{0:T(1024)S(1)}, f32[]{:T(128)}, f32[448,3584]{1,0:T(8,128)}) fusion(s32[3584]{0:T(1024)S(1)} %iota_add_fusion, s32[448]{0:T(512)S(1)} %iota_add_fusion.1, bf16[2048,448]{1,0:T(8,128)(2,1)} %all-reduce.2.cloned.1.call-done, bf16[2048,3584]{1,0:T(8,128)(2,1)} %all-gather.2.cloned.1.call-done), kind=kOutput, calls=%fused_computation.6 | convolution fusion | flops 6586298880 | bytes 22968068 | tf_op jit(solution)/shard_map/dot_general | solution.py:50
  738.4 53.1 %pmax.14 = f32[3584]{0:T(1024)S(1)} all-reduce(f32[3584]{0:T(1024)S(1)} %get-tuple-element.3), channel_id=1, replica_groups=mesh['tok'=16,'blk'=2] {'tok'}, use_global_device_ids=true, to_apply=%region_4.5 | all-reduce | flops 3584 | bytes 28672 | tf_op jit(solution)/shard_map/pmax | solution.py:82
  791.5 48.2 %psum.15 = f32[]{:T(128)} all-reduce(f32[]{:T(128)} %get-tuple-element.4), channel_id=1, replica_groups=mesh['tok'=16,'blk'=2] {'tok','blk'}, use_global_device_ids=true, to_apply=%region_2.3 | all-reduce | flops 1 | bytes 8 | tf_op jit(solution)/shard_map/psum | solution.py:83
  840.4 1.2 fusion.11
  841.6 5.5 pmax.15
  847.1 6.5 fusion.1
  (9 shorter events, 0.1 us)
Async XLA Ops:
  7.2 651.0 %all-gather.2.cloned.1.call-start = ((), (), s32[]{:S(2)}) async-start(), calls=%async_computation | async-start | bytes 15597568 | tf_op jit(solution)/shard_map/all_gather | solution.py:71
  149.9 326.1 %copy-start.1 = (f32[3584]{0:T(1024)S(1)}, f32[3584]{0:T(1024)}, u32[]{:S(2)}) copy-start(f32[3584]{0:T(1024)} %param.3) | copy-start | bytes 43012
  149.9 326.1 %copy-start = (bf16[128,3584]{1,0:T(8,128)(2,1)S(1)}, bf16[128,3584]{1,0:T(8,128)(2,1)}, u32[]{:S(2)}) copy-start(bf16[128,3584]{1,0:T(8,128)(2,1)} %param.2) | copy-start | bytes 2752516
  500.3 41.9 %collective-permute-start = (f32[128,3584]{1,0:T(8,128)S(1)}, f32[128,3584]{1,0:T(8,128)}, u32[]{:S(2)}, u32[]{:S(2)}) collective-permute-start(f32[128,3584]{1,0:T(8,128)S(1)} %fusion.3), channel_id=1, source_target_pairs={{0,1},{1,0},{2,3},{3,2},{4,5},{5,4},{6,7},{7,6},{8,9},{9,8},{10,11... | collective-permute-start | bytes 5505032 | tf_op jit(solution)/shard_map/ppermute | solution.py:24
  545.0 179.4 %all-reduce.2.cloned.1.call-start = ((), (), s32[]{:S(2)}) async-start(), calls=%async_computation.1 | async-start | bytes 4194304 | tf_op jit(solution)/shard_map/psum | solution.py:29
Sparse Core Ops, SparseCore 0:
  545.1 113.0 all-gather.1
  662.7 61.6 all-reduce.1
where the time goes:
time: 867 us; the launch traced here: 860 us
  local copies, waits for them, and re-layouts  326 us (38%)
  waiting for transfers between devices  216 us (25%)
  other arithmetic  157 us (18%)
  blocking collectives  107 us (12%)
  matrix products  38.4 us (4%)
  between operations  14.8 us (2%)
    mul x1, local copies, waits for them, and re-layouts, per_device(): jnp.kron(walsh_table(local_walsh) / math.sqrt(local_walsh), cosine_table(...  326 us
    mul x1, other arithmetic, per_device(): jnp.kron(walsh_table(local_walsh) / math.sqrt(local_walsh), cosine_table(...  142 us
    all_gather x1, waiting for transfers between devices, per_device(): all_tokens = lax.all_gather(rotated, 'tok', axis=0, tiled=True)  113 us
    psum x1, waiting for transfers between devices, from_root(): return lax.psum(kept, axis)  61.7 us
    pmax x1, blocking collectives, per_device(): column_peak = lax.pmax(local_peaks, 'tok')  53.1 us
    psum x1, blocking collectives, per_device(): lax.psum(jnp.sum(jnp.where(on_diag, gram_block, 0.0)), ('tok', 'blk'))  48.2 us
    ppermute x1, waiting for transfers between devices, swapped(): return lax.ppermute(block, axis, route)  41.4 us
    dot_general x1, matrix products, per_device(): jnp.dot(signed.astype(jnp.float32), local_table, precision=lax.Precision....  24.3 us
  transfers between devices with their start and end apart: 3, of which 3 were waited for; matrix products, arithmetic and copies ran while one was open for 0% of the time, Pallas kernels for 0%

commit v1 on v0

v1 whole, which is shorter than its diff:
```python
import math

import jax
import jax.numpy as jnp
import numpy as np
from jax import lax
from jax.sharding import PartitionSpec as P

WALSH = 512
MIX = 14
EPS = 1e-06
DAMP = 0.01
LANES = 128


def walsh_np(order):
    index = np.arange(order)
    parity = np.zeros((order, order), np.int64)
    for bit in range(order.bit_length() - 1):
        parity += (index[:, None] >> bit & 1) * (index[None, :] >> bit & 1)
    return (1 - 2 * (parity % 2)).astype(np.float64)


def cosine_np(order):
    k = np.arange(order, dtype=np.float64)[:, None]
    n = np.arange(order, dtype=np.float64)[None, :]
    table = math.sqrt(2.0 / order) * np.cos(math.pi * (n + 0.5) * k / order)
    table[0] *= math.sqrt(0.5)
    return table


def walsh_jnp(order):
    index = jnp.arange(order, dtype=jnp.int32)
    joint = index[:, None] & index[None, :]
    for bit in (16, 8, 4, 2, 1):
        joint = joint ^ (joint >> bit)
    return (1 - 2 * (joint & 1)).astype(jnp.float32)


def inner_tables(inner):
    cos = (cosine_np(MIX).T / math.sqrt(WALSH)).astype(np.float32)
    high = np.asarray(cos.astype(jnp.bfloat16))
    low = np.asarray((cos - high.astype(np.float32)).astype(jnp.bfloat16))
    walsh = walsh_jnp(inner).astype(jnp.bfloat16)
    tables = []
    for part in (high, low):
        rows = jnp.repeat(jnp.repeat(walsh, MIX, axis=0), MIX, axis=1)
        tables.append(rows * jnp.tile(jnp.asarray(part), (inner, inner)))
    return tables


def pair_route(count, step):
    return [(i, i ^ step) for i in range(count)]


def per_device(activations, signs):
    tokens, width = activations.shape
    blocks = lax.axis_size("blk")
    blk = lax.axis_index("blk")
    groups = lax.axis_size("tok")
    tok = lax.axis_index("tok")
    features = width * blocks
    inner = math.gcd(width // MIX, WALSH // blocks, 64)
    inner_width = inner * MIX
    outer = width // inner_width

    signed = activations * signs.astype(jnp.bfloat16)[None, :]
    tables = inner_tables(inner)

    def spread(part):
        stacked = jnp.concatenate(
            [part[:, i * inner_width : (i + 1) * inner_width] for i in range(outer)], axis=0
        )
        mixed = sum(jnp.dot(stacked, t, preferred_element_type=jnp.float32) for t in tables)
        parts = [mixed[i * tokens : (i + 1) * tokens] for i in range(outer)]
        step = 1
        while step < outer:
            parts = [
                parts[i ^ step] - parts[i] if i & step else parts[i] + parts[i ^ step]
                for i in range(outer)
            ]
            step *= 2
        return jnp.concatenate(parts, axis=1)

    total = None
    for step in range(blocks):
        block = signed if step == 0 else lax.ppermute(signed, "blk", pair_route(blocks, step))
        joint = blk & (blk ^ step)
        parity = sum(joint >> bit & 1 for bit in range(max(1, blocks.bit_length() - 1))) & 1
        sign = jnp.where(parity == 1, -1.0, 1.0).astype(jnp.float32)
        term = spread(block) * sign
        total = term if total is None else total + term
    rotated = total.astype(jnp.bfloat16)

    wide = rotated.astype(jnp.float32)
    trace_total = jnp.sum(wide * wide, axis=0, keepdims=True).reshape(-1, LANES)
    trace_total = jnp.sum(trace_total, axis=0)
    for axis, count in (("blk", blocks), ("tok", groups)):
        step = 1
        while step < count:
            trace_total += lax.ppermute(trace_total, axis, pair_route(count, step))
            step *= 2
    trace_total = jnp.sum(trace_total)
    diag_mean = trace_total / features + EPS

    all_tokens = lax.all_gather(rotated, "tok", axis=0, tiled=True)
    row_count = features // groups
    owner = tok * row_count // width
    offset = tok * row_count - owner * width
    own_slice = lax.dynamic_slice_in_dim(all_tokens, offset, row_count, 1)
    row_slice = jnp.where(blk == owner, own_slice, 0).astype(jnp.bfloat16)
    for step in range(1, blocks):
        route = []
        for t in range(groups):
            source = t * row_count // width
            route.append((t * blocks + source, t * blocks + (source ^ step)))
        row_slice = row_slice + lax.ppermute(own_slice, ("tok", "blk"), route)

    gram = lax.dot_general(
        row_slice, all_tokens, (((0,), (0,)), ((), ())), preferred_element_type=jnp.float32
    )
    rows = tok * row_count + jnp.arange(row_count, dtype=jnp.int32)[:, None]
    columns = blk * width + jnp.arange(width, dtype=jnp.int32)[None, :]
    on_diag = rows == columns
    row_peak = jnp.max(jnp.where(on_diag, 0.0, jnp.abs(gram)), axis=1)
    hessian = gram / diag_mean + DAMP * on_diag.astype(jnp.float32)
    step = 1
    while step < blocks:
        row_peak = jnp.maximum(row_peak, lax.ppermute(row_peak, "blk", pair_route(blocks, step)))
        step *= 2
    peaks = row_peak[None, :]
    step = 1
    while step < groups:
        other = lax.ppermute(peaks, "tok", pair_route(groups, step))
        upper = (tok & step) != 0
        peaks = jnp.concatenate(
            [jnp.where(upper, other, peaks), jnp.where(upper, peaks, other)], axis=0
        )
        step *= 2
    peaks = peaks.reshape(features)
    incoherence = lax.dynamic_slice_in_dim(peaks, blk * width, width, 0) / diag_mean
    return hessian, incoherence, jnp.max(peaks) / diag_mean


def solution(mesh):
    in_specs = (P("tok", "blk"), P("blk"))
    out_specs = (P("tok", "blk"), P("blk"), P())
    return jax.shard_map(
        per_device, mesh=mesh, in_specs=in_specs, out_specs=out_specs, check_vma=False
    )
```

time: 867 us -> 317 us (0.37)
  local copies, waits for them, and re-layouts: 326 us -> 79.5 us
  other arithmetic: 157 us -> 5.55 us
  blocking collectives: 107 us -> 0 us
  waiting for transfers between devices: 216 us -> 177 us
  matrix products: 38.4 us -> 24.3 us
  starting transfers between devices: 0.83 us -> 11.2 us
    mul x1 -> x0, local copies, waits for them, and re-layouts: 326 us -> none  [per_device(): jnp.kron(walsh_table(local_walsh) / math.sqrt(local_walsh), cosine_table(...]
    mul x2 -> x1, other arithmetic: 142 us -> 1.24 us  [per_device(): signed = activations * signs.astype(jnp.bfloat16)[None, :]]
    another operation x0 -> x6, local copies, waits for them, and re-layouts: none -> 65.6 us  [inner_tables(): tables.append(rows * jnp.tile(jnp.asarray(part), (inner, inner)))]
    psum x1 -> x0, waiting for transfers between devices: 61.7 us -> none  [from_root(): return lax.psum(kept, axis)]
    pmax x2 -> x0, blocking collectives: 58.6 us -> none  [the longest x1 53.1 us: per_device(): column_peak = lax.pmax(local_peaks, 'tok')]
    psum x1 -> x0, blocking collectives: 48.2 us -> none  [per_device(): lax.psum(jnp.sum(jnp.where(on_diag, gram_block, 0.0)), ('tok', 'blk'))]
    ppermute x1 -> x12, waiting for transfers between devices: 41.4 us -> 63.4 us  [the longest x5 49.5 us: per_device(): trace_total += lax.ppermute(trace_total, axis, pair_route(count, step))]
    dot_general x2 -> x5, matrix products: 38.4 us -> 24.3 us  [the longest x1 13.6 us: per_device(): lax.dot_general(row_slice, all_tokens, (((0,), (0,)), ((), ())), preferre...]
  transfers between devices with their start and end apart: 3 -> 13, of which waited for: 3 -> 11; matrix products, arithmetic and copies ran while one was open for 0% -> 25% of each run, Pallas kernels for 0% -> 0%
where the time goes in v1:
time: 317 us; the launch traced here: 314 us
  waiting for transfers between devices  177 us (56%)
  local copies, waits for them, and re-layouts  79.5 us (25%)
  matrix products  24.3 us (8%)
  between operations  17.4 us (5%)
  starting transfers between devices  11.2 us (4%)
  other arithmetic  5.55 us (2%)
    all_gather x1, waiting for transfers between devices, per_device(): all_tokens = lax.all_gather(rotated, 'tok', axis=0, tiled=True)  113 us
    another operation x6, local copies, waits for them, and re-layouts, inner_tables(): tables.append(rows * jnp.tile(jnp.asarray(part), (inner, inner)))  65.6 us
    ppermute x5, waiting for transfers between devices, per_device(): trace_total += lax.ppermute(trace_total, axis, pair_route(count, step))  49.5 us
    dot_general x1, matrix products, per_device(): lax.dot_general(row_slice, all_tokens, (((0,), (0,)), ((), ())), preferre...  13.6 us
    dot_general x4, matrix products, spread(): jnp.dot(stacked, t, preferred_element_type=jnp.float32)  10.6 us
    ppermute x4, waiting for transfers between devices, per_device(): other = lax.ppermute(peaks, 'tok', pair_route(groups, step))  10.3 us
  transfers between devices with their start and end apart: 13, of which 11 were waited for; matrix products, arithmetic and copies ran while one was open for 25% of the time, Pallas kernels for 0%

profile of v1, /device:TPU:12, one launch (start us, length us, event | category | flops | bytes accessed | tf_op | source)
XLA Modules:
  0.0 314.5 jit_solution(6557556047697496267)
XLA Ops:
  7.2 0.7 convert_element_type.22
  7.9 1.2 broadcast_multiply_fusion
  9.2 0.6 collective-permute-start
  9.8 0.8 fusion.36
  10.7 0.1 copy.15
  10.8 0.1 broadcast_in_dim.27
  11.0 1.4 reshape.35
  12.4 8.8 %tile.8 = bf16[64,14,64,14]{3,2,1,0:T(8,128)(2,1)} broadcast(bf16[14,14]{1,0:T(8,128)(2,1)S(1)} %copy-done.5), dimensions={1,3} | broadcast | bytes 1606024 | tf_op jit(solution)/shard_map/tile | solution.py:48
  21.3 21.6 %tile.9 = bf16[896,896]{1,0:T(8,128)(2,1)S(1)} reshape(bf16[64,14,64,14]{3,2,1,0:T(8,128)(2,1)} %tile.8) | data formatting | bytes 3211264 | tf_op jit(solution)/shard_map/tile | solution.py:48
  42.9 2.3 copy.16
  45.2 4.4 %fusion.13 = f32[512,896]{1,0:T(8,128)} fusion(bf16[896,896]{0,1:T(8,128)(2,1)} %reshape.35, bf16[896,896]{0,1:T(8,128)(2,1)} %copy.16, bf16[128,896]{1,0:T(8,128)(2,1)S(1)} %get-tuple-element.20, bf16[128,896]{1,0:T(8,128)(2,1)S(1)} %get-tuple-element.21, bf16[128,896]{1,0:T(8,128)(2,1)S(1)} %copy-done.3, bf16[128,896]{1,0:T(8,128)(2,1)S(1)} %get-tuple-element.19), kind=kOutput, calls=%fused_computation.22 | convolution fusion | flops 826556416 | bytes 5963776 | tf_op jit(solution)/shard_map/dot_general | solution.py:74
  49.6 8.8 %tile.20 = bf16[64,14,64,14]{3,2,1,0:T(8,128)(2,1)} broadcast(bf16[14,14]{1,0:T(8,128)(2,1)S(1)} %copy-done.4), dimensions={1,3} | broadcast | bytes 1606024 | tf_op jit(solution)/shard_map/tile | solution.py:48
  58.5 21.6 %tile.21 = bf16[896,896]{1,0:T(8,128)(2,1)S(1)} reshape(bf16[64,14,64,14]{3,2,1,0:T(8,128)(2,1)} %tile.20) | data formatting | bytes 3211264 | tf_op jit(solution)/shard_map/tile | solution.py:48
  80.1 2.3 copy.17
  82.4 3.7 %convolution_add_fusion.1 = f32[512,896]{1,0:T(8,128)S(1)} fusion(f32[512,896]{1,0:T(8,128)} %fusion.13, bf16[896,896]{0,1:T(8,128)(2,1)} %reshape.35, bf16[896,896]{0,1:T(8,128)(2,1)} %copy.17, bf16[128,896]{1,0:T(8,128)(2,1)S(1)} %get-tuple-element.20, bf16[128,896]{1,0:T(8,128)(2,1)S(1)} %get-tuple-element.21, bf16[128,896]{1,0:T(8,128)(2,1)S(1)} %copy-done.3, ...), kind=kOutput, calls=%fused_computation.14 | convolution fusion | flops 827015168 | bytes 7798784 | tf_op jit(solution)/shard_map/dot_general | solution.py:74
  86.2 0.2 fusion.16
  86.3 1.5 fusion.37
  88.0 0.5 copy-done.1
  88.5 1.3 fusion.9
  89.8 0.1 copy-done
  89.9 1.3 convolution_add_fusion
  91.2 0.2 fusion.20
  91.3 1.3 multiply_reduce_fusion
  92.7 113.2 %all-gather.2.cloned.1.call-done = bf16[2048,3584]{1,0:T(8,128)(2,1)} async-done(((bf16[128,3584]{1,0:T(8,128)(2,1)}), bf16[2048,3584]{1,0:T(8,128)(2,1)}) %all-gather.2.cloned.1.call-update) | async-done | bytes 14680080 | tf_op jit(solution)/shard_map/all_gather | solution.py:106
  205.9 2.8 constant_dynamic-slice_fusion
  208.7 2.3 copy.18
  211.0 1.3 collective-permute-start.1
  212.3 4.0 %collective-permute-start.2 = (f32[128]{0:T(128)S(1)}, f32[128]{0:T(128)S(1)}, u32[]{:S(2)}, u32[]{:S(2)}) collective-permute-start(f32[128]{0:T(128)S(1)} %bitcast_reduce_fusion), channel_id=1, source_target_pairs={{0,1},{1,0},{2,3},{3,2},{4,5},{5,4},{6,7},{7,6},{8,9},{9,8},{10,11... | collective-permute-start | bytes 1544 | tf_op jit(solution)/shard_map/ppermute | solution.py:101
  216.3 39.1 %collective-permute-done.2 = f32[128]{0:T(128)S(1)} collective-permute-done((f32[128]{0:T(128)S(1)}, f32[128]{0:T(128)S(1)}, u32[]{:S(2)}, u32[]{:S(2)}) %collective-permute-start.2) | collective-permute-done | bytes 544 | tf_op jit(solution)/shard_map/ppermute | solution.py:101
  255.4 1.2 collective-permute-done.3
  256.5 0.4 collective-permute-start.4
  256.9 3.2 %collective-permute-done.4 = f32[128]{0:T(128)S(1)} collective-permute-done((f32[128]{0:T(128)S(1)}, f32[128]{0:T(128)S(1)}, u32[]{:S(2)}, u32[]{:S(2)}) %collective-permute-start.4) | collective-permute-done | bytes 544 | tf_op jit(solution)/shard_map/ppermute | solution.py:101
  260.1 1.9 collective-permute-start.5
  262.0 1.6 collective-permute-done.5
  263.7 4.5 %collective-permute-done.6 = f32[128]{0:T(128)S(1)} collective-permute-done((f32[128]{0:T(128)S(1)}, f32[128]{0:T(128)S(1)}, u32[]{:S(2)}, u32[]{:S(2)}) %collective-permute-start.6) | collective-permute-done | bytes 544 | tf_op jit(solution)/shard_map/ppermute | solution.py:101
  268.1 0.6 add_reduce_fusion
  269.4 3.8 %copy.19 = bf16[2048,448]{1,0:T(8,128)(2,1)} copy(bf16[2048,448]{0,1:T(8,128)(2,1)} %collective-permute-done.1) | data formatting | bytes 3670016 | tf_op jit(solution)/shard_map/ppermute | solution.py:117
  273.2 13.6 %fusion.1 = (f32[448]{0:T(512)S(1)}, f32[448,3584]{1,0:T(8,128)}) fusion(s32[3584]{0:T(1024)S(1)} %iota_add_fusion, s32[448]{0:T(512)S(1)} %iota_add_fusion.1, f32[]{:T(128)S(6)} %add.104, bf16[2048,3584]{1,0:T(8,128)(2,1)} %all-gather.2.cloned.1.call-done, bf16[2048,448]{1,0:T(8,128)(2,1)} %copy.19, bf16[2048,448]{1,0:T(8,128)(2,1)S(1)} %constant_dynamic-slice_fusion, ...), kind=kOutput, calls=%fused_computation.3 | convolution fusion | flops 6589742592 | bytes 24790532 | tf_op jit(solution)/shard_map/dot_general | solution.py:119
  286.9 3.6 %collective-permute-done.7 = f32[448]{0:T(512)S(1)} collective-permute-done((f32[448]{0:T(512)S(1)}, f32[448]{0:T(512)S(1)}, u32[]{:S(2)}, u32[]{:S(2)}) %collective-permute-start.7) | collective-permute-done | bytes 1824 | tf_op jit(solution)/shard_map/ppermute | solution.py:129
  290.5 1.2 collective-permute-done.8
  291.6 0.5 collective-permute-start.9
  292.2 3.2 %collective-permute-done.9 = f32[2,448]{1,0:T(2,128)S(1)} collective-permute-done((f32[2,448]{1,0:T(2,128)S(1)}, f32[2,448]{1,0:T(2,128)S(1)}, u32[]{:S(2)}, u32[]{:S(2)}) %collective-permute-start.9) | collective-permute-done | bytes 3616 | tf_op jit(solution)/shard_map/ppermute | solution.py:134
  295.3 2.0 collective-permute-start.10
  297.3 1.7 collective-permute-done.10
  299.1 0.5 collective-permute-start.11
  299.6 4.2 %collective-permute-done.11 = f32[8,448]{1,0:T(8,128)S(1)} collective-permute-done((f32[8,448]{1,0:T(8,128)S(1)}, f32[8,448]{1,0:T(8,128)S(1)}, u32[]{:S(2)}, u32[]{:S(2)}) %collective-permute-start.11) | collective-permute-done | bytes 14368 | tf_op jit(solution)/shard_map/ppermute | solution.py:134
  303.8 0.6 fusion.34
  305.8 0.7 dynamic-slice_divide_fusion
  (37 shorter events, 0.6 us)
Async XLA Ops:
  7.2 198.7 %all-gather.2.cloned.1.call-start = ((), (), s32[]{:S(2)}) async-start(), calls=%async_computation | async-start | bytes 15597568 | tf_op jit(solution)/shard_map/all_gather | solution.py:106
  9.2 77.1 %collective-permute-start = (bf16[128,3584]{1,0:T(8,128)(2,1)S(1)}, bf16[128,3584]{1,0:T(8,128)(2,1)}, u32[]{:S(2)}, u32[]{:S(2)}) collective-permute-start(bf16[128,3584]{1,0:T(8,128)(2,1)S(1)} %broadcast_multiply_fusion), channel_id=1, source_target_pairs={{0,1},{1,0},{2,3},{3,2},{4,5},{5,4},{6,7},{7,6},{8,9},{9,8},{10,11... | collective-permute-start | bytes 2752520 | tf_op jit(solution)/shard_map/ppermute | solution.py:87
  11.0 1.4 copy-start.5
  42.9 2.4 copy-start.3
  45.2 4.4 %copy-start.4 = (bf16[14,14]{1,0:T(8,128)(2,1)S(1)}, bf16[14,14]{1,0:T(8,128)(2,1)}, u32[]{:S(2)}) copy-start(bf16[14,14]{1,0:T(8,128)(2,1)} %constant.60.clone) | copy-start | bytes 1180
  86.1 1.8 copy-start.2
  86.3 2.2 copy-start.1
  88.5 1.4 copy-start
  211.0 58.4 %collective-permute-start.1 = (bf16[2048,448]{0,1:T(8,128)(2,1)}, bf16[2048,448]{0,1:T(8,128)(2,1)}, u32[]{:S(2)}, u32[]{:S(2)}) collective-permute-start(bf16[2048,448]{0,1:T(8,128)(2,1)} %copy.18), channel_id=1, source_target_pairs={{0,1},{2,3},{4,5},{6,7},{8,9},{10,11},{12,13},{14,15},{17,16},{19,... | collective-permute-start | bytes 5505032 | tf_op jit(solution)/shard_map/ppermute | solution.py:117
  212.3 43.1 %collective-permute-start.2 = (f32[128]{0:T(128)S(1)}, f32[128]{0:T(128)S(1)}, u32[]{:S(2)}, u32[]{:S(2)}) collective-permute-start(f32[128]{0:T(128)S(1)} %bitcast_reduce_fusion), channel_id=1, source_target_pairs={{0,1},{1,0},{2,3},{3,2},{4,5},{5,4},{6,7},{7,6},{8,9},{9,8},{10,11... | collective-permute-start | bytes 1544 | tf_op jit(solution)/shard_map/ppermute | solution.py:101
  255.4 1.2 collective-permute-start.3
  256.5 3.6 %collective-permute-start.4 = (f32[128]{0:T(128)S(1)}, f32[128]{0:T(128)S(1)}, u32[]{:S(2)}, u32[]{:S(2)}) collective-permute-start(f32[128]{0:T(128)S(1)} %add.100), channel_id=1, source_target_pairs={{0,4},{2,6},{4,0},{6,2},{8,12},{10,14},{12,8},{14,10},{16,20},{18,... | collective-permute-start | bytes 1544 | tf_op jit(solution)/shard_map/ppermute | solution.py:101
  260.1 3.6 %collective-permute-start.5 = (f32[128]{0:T(128)S(1)}, f32[128]{0:T(128)S(1)}, u32[]{:S(2)}, u32[]{:S(2)}) collective-permute-start(f32[128]{0:T(128)S(1)} %add.101), channel_id=1, source_target_pairs={{0,8},{2,10},{4,12},{6,14},{8,0},{10,2},{12,4},{14,6},{16,24},{18,... | collective-permute-start | bytes 1544 | tf_op jit(solution)/shard_map/ppermute | solution.py:101
  263.7 4.5 %collective-permute-start.6 = (f32[128]{0:T(128)S(1)}, f32[128]{0:T(128)S(1)}, u32[]{:S(2)}, u32[]{:S(2)}) collective-permute-start(f32[128]{0:T(128)S(1)} %add.102), channel_id=1, source_target_pairs={{0,16},{2,18},{4,20},{6,22},{8,24},{10,26},{12,28},{14,30},{16,0},... | collective-permute-start | bytes 1544 | tf_op jit(solution)/shard_map/ppermute | solution.py:101
  286.9 3.6 %collective-permute-start.7 = (f32[448]{0:T(512)S(1)}, f32[448]{0:T(512)S(1)}, u32[]{:S(2)}, u32[]{:S(2)}) collective-permute-start(f32[448]{0:T(512)S(1)} %get-tuple-element.9), channel_id=1, source_target_pairs={{0,1},{1,0},{2,3},{3,2},{4,5},{5,4},{6,7},{7,6},{8,9},{9,8},{10,11... | collective-permute-start | bytes 5384 | tf_op jit(solution)/shard_map/ppermute | solution.py:129
  290.4 1.2 collective-permute-start.8
  291.6 3.7 %collective-permute-start.9 = (f32[2,448]{1,0:T(2,128)S(1)}, f32[2,448]{1,0:T(2,128)S(1)}, u32[]{:S(2)}, u32[]{:S(2)}) collective-permute-start(f32[2,448]{1,0:T(2,128)S(1)} %pad_maximum_fusion.9), channel_id=1, source_target_pairs={{0,4},{2,6},{4,0},{6,2},{8,12},{10,14},{12,8},{14,10},{16,20},{18,... | collective-permute-start | bytes 10760 | tf_op jit(solution)/shard_map/ppermute | solution.py:134
  295.3 3.7 %collective-permute-start.10 = (f32[4,448]{1,0:T(4,128)S(1)}, f32[4,448]{1,0:T(4,128)S(1)}, u32[]{:S(2)}, u32[]{:S(2)}) collective-permute-start(f32[4,448]{1,0:T(4,128)S(1)} %pad_maximum_fusion.8), channel_id=1, source_target_pairs={{0,8},{2,10},{4,12},{6,14},{8,0},{10,2},{12,4},{14,6},{16,24},{18,... | collective-permute-start | bytes 21512 | tf_op jit(solution)/shard_map/ppermute | solution.py:134
  299.1 4.7 %collective-permute-start.11 = (f32[8,448]{1,0:T(8,128)S(1)}, f32[8,448]{1,0:T(8,128)S(1)}, u32[]{:S(2)}, u32[]{:S(2)}) collective-permute-start(f32[8,448]{1,0:T(8,128)S(1)} %pad_maximum_fusion.7), channel_id=1, source_target_pairs={{0,16},{2,18},{4,20},{6,22},{8,24},{10,26},{12,28},{14,30},{16,0},... | collective-permute-start | bytes 43016 | tf_op jit(solution)/shard_map/ppermute | solution.py:134
Sparse Core Ops, SparseCore 0:
  92.7 113.1 all-gather.1
